TPU v7x, 32 devices: a whole 2x2x4 slice. The times are simulated.
32 devices in a mesh: batch: 4 (over y, core), tm: 2 (over x), space: 4 (over z).
Axes of the slice: x: 2, y: 2, z: 4, core: 2. Of those that a mesh axis runs over, the one named last changes fastest.
Arguments:
- clip_tokens: bfloat16 [4, 4, 32, 32, 1024], P('batch', None, 'space', 'tm'), may hold values from -6 to 6
- frame_order: int32 [4, 4], P('batch'), may hold values from 0 to 3, each once within a row
- row_reach: int32 [4, 4], P('batch', 'tm'), may hold values from 1 to 4
- spatial_gain: float32 [1024], replicated, may hold values from 0.1 to 1.9
- spatial_heads: bfloat16 [1024, 3072], replicated, may hold values from -2 to 2
- spatial_merge: bfloat16 [1024, 1024], replicated, may hold values from -0.1875 to 0.1875
- temporal_gain: float32 [1024], replicated, may hold values from 0.1 to 1.9
- temporal_heads: bfloat16 [1024, 3072], replicated, may hold values from -2 to 2
- temporal_merge: bfloat16 [1024, 1024], replicated, may hold values from -0.1875 to 0.1875
- cotangent: bfloat16 [4, 4, 32, 32, 1024], P('batch', 'tm', 'space'), may hold values from -0.059814453 to 0.059814453
Outputs:
- output: bfloat16 [4, 4, 32, 32, 1024], P('batch', 'tm', 'space')
- weight_grad: float32 [1024, 1024], P(('tm', 'space'))
Inputs may be any that keep to these rules, and one draw needn't show every extreme that they name: Each row of frame_order names every number from 0 to 3 once.
All inputs are finite; a program needn't handle non-finite values.
Results may differ from a plain program's by a relative error of at most 0.025.
Values may be sent and summed in bfloat16 or wider, within the bound.
A program may use at most 128 MiB of HBM per device.

v0:
```python
import jax
import jax.numpy as jnp
from jax import lax
from jax.sharding import PartitionSpec as P

HALO = 4
D = 1024
HEADS = 16
HEAD_DIM = 64
floor_term = 0.5


def extended(value, sides, width):
    for axis, dim in sides:
        devices, length = (lax.axis_size(axis), value.shape[dim])
        up = [(i, (i + 1) % devices) for i in range(devices - 1)]
        down = [(j, i) for i, j in up]
        last = lax.slice_in_dim(value, length - width, length, axis=dim)
        initial = lax.slice_in_dim(value, 0, width, axis=dim)
        before = lax.ppermute(last, axis, up)
        after = lax.ppermute(initial, axis, down)
        value = jnp.concatenate([before, value, after], axis=dim)
    return value


def normalize(values, gain_vector):
    widened = values.astype(jnp.float32)
    scaled = widened * lax.rsqrt(jnp.mean(widened * widened, axis=-1, keepdims=True) + floor_term)
    return (scaled * gain_vector).astype(jnp.bfloat16)


def softmax_rounded(scores, allowed):
    masked = jnp.where(allowed, scores, -1e30)
    top_score = jnp.max(masked, axis=-1, keepdims=True)
    exponent = jnp.exp(masked - top_score)
    return (exponent / jnp.sum(exponent, axis=-1, keepdims=True)).astype(jnp.bfloat16)


def temporal_attend(queries, keys_all, values_all, query_order, key_order):
    clip_count, query_frames, positions, _ = queries.shape
    key_frames = keys_all.shape[1]
    query_heads = queries.reshape(clip_count, query_frames, positions, HEADS, HEAD_DIM)
    key_heads = keys_all.reshape(clip_count, key_frames, positions, HEADS, HEAD_DIM)
    value_heads = values_all.reshape(clip_count, key_frames, positions, HEADS, HEAD_DIM)
    scores = jnp.einsum(
        "cfthd,cgthd->cthfg", query_heads, key_heads, preferred_element_type=jnp.float32
    ) * HEAD_DIM ** (-0.5)
    allowed = key_order[:, None, :] <= query_order[:, :, None]
    weights = softmax_rounded(scores, allowed[:, None, None])
    context = jnp.einsum(
        "cthfg,cgthd->cfthd", weights, value_heads, preferred_element_type=jnp.float32
    )
    return context.reshape(clip_count, query_frames, positions, D).astype(jnp.bfloat16)


def per_device(
    clip_tokens,
    frame_order,
    row_reach,
    spatial_gain,
    spatial_heads,
    spatial_merge,
    temporal_gain,
    temporal_heads,
    temporal_merge,
    cotangent,
):
    frames_here = lax.all_to_all(clip_tokens, "tm", split_axis=1, concat_axis=3, tiled=True)
    clip_count, frame_count, row_count, col_count, _ = frames_here.shape
    tokens = row_count * col_count
    normed = normalize(frames_here, spatial_gain)
    projected = jnp.dot(normed, spatial_heads, preferred_element_type=jnp.float32).astype(
        jnp.bfloat16
    )
    key_value = extended(projected[..., D:], (("space", 2),), HALO)
    extent = (row_count + 2 * HALO) * col_count
    first_row = lax.axis_index("space") * row_count
    all_rows = row_count * lax.axis_size("space")
    query_rows = first_row + jnp.arange(tokens, dtype=jnp.int32) // col_count
    key_rows = first_row - HALO + jnp.arange(extent, dtype=jnp.int32) // col_count
    inside = (key_rows >= 0) & (key_rows < all_rows)
    distance = jnp.abs(key_rows[None, :] - query_rows[:, None])

    def spatial_item(inputs):
        queries, key_pairs, reach_now = inputs
        query_heads = queries.reshape(tokens, HEADS, HEAD_DIM)
        key_heads = key_pairs[:, :D].reshape(extent, HEADS, HEAD_DIM)
        value_heads = key_pairs[:, D:].reshape(extent, HEADS, HEAD_DIM)
        scores = jnp.einsum(
            "qhd,khd->hqk", query_heads, key_heads, preferred_element_type=jnp.float32
        ) * HEAD_DIM ** (-0.5)
        allowed = inside[None, :] & (distance <= reach_now)
        weights = softmax_rounded(scores, allowed[None])
        context = jnp.einsum(
            "hqk,khd->qhd", weights, value_heads, preferred_element_type=jnp.float32
        )
        return context.reshape(tokens, D).astype(jnp.bfloat16)

    item_count = clip_count * frame_count
    spatial_context = lax.map(
        spatial_item,
        (
            projected[..., :D].reshape(item_count, tokens, D),
            key_value.reshape(item_count, extent, 2 * D),
            row_reach.reshape(item_count),
        ),
    )
    flat_input = frames_here.reshape(clip_count, frame_count, tokens, D)
    spatial_context = spatial_context.reshape(clip_count, frame_count, tokens, D)
    middle = (
        flat_input.astype(jnp.float32)
        + jnp.dot(spatial_context, spatial_merge, preferred_element_type=jnp.float32)
    ).astype(jnp.bfloat16)
    normed_two = normalize(middle, temporal_gain)
    projected_two = jnp.dot(normed_two, temporal_heads, preferred_element_type=jnp.float32).astype(
        jnp.bfloat16
    )
    regrouped = lax.all_to_all(projected_two, "tm", split_axis=2, concat_axis=1, tiled=True)
    context_all = temporal_attend(
        regrouped[..., :D],
        regrouped[..., D : 2 * D],
        regrouped[..., 2 * D :],
        frame_order,
        frame_order,
    )
    temporal_context = lax.all_to_all(context_all, "tm", split_axis=1, concat_axis=2, tiled=True)
    output = (
        middle.astype(jnp.float32)
        + jnp.dot(temporal_context, temporal_merge, preferred_element_type=jnp.float32)
    ).astype(jnp.bfloat16)
    flat_context = temporal_context.reshape(-1, D)
    flat_cotangent = cotangent.reshape(-1, D)
    own_rows = lax.psum_scatter(
        lax.dot_general(
            flat_context,
            flat_cotangent,
            (((0,), (0,)), ((), ())),
            preferred_element_type=jnp.float32,
        ).astype(jnp.bfloat16),
        ("tm", "space"),
        scatter_dimension=0,
        tiled=True,
    )
    weight_grad = lax.psum(own_rows, "batch").astype(jnp.float32)
    return (output.reshape(clip_count, frame_count, row_count, col_count, D), weight_grad)


def solution(mesh):
    in_specs = (
        P("batch", None, "space", "tm", None),
        P("batch", None),
        P("batch", "tm"),
        P(),
        P(),
        P(),
        P(),
        P(),
        P(),
        P("batch", "tm", "space", None, None),
    )
    out_specs = (P("batch", "tm", "space", None, None), P(("tm", "space"), None))
    return jax.shard_map(
        per_device, mesh=mesh, in_specs=in_specs, out_specs=out_specs, check_vma=False
    )
```

profile of v0, /device:TPU:0, one launch (start us, length us, event | category | flops | bytes accessed | tf_op | source)
XLA Modules:
  0.0 350.0 jit_solution(2444274592889547098)
XLA Ops:
  7.2 18.8 %all_to_all.42 = bf16[1,4,8,16,1024]{4,3,2,0,1:T(8,128)(2,1)S(1)} all-to-all(bf16[1,4,8,16,1024]{4,3,2,0,1:T(8,128)(2,1)} %bitcast.124), channel_id=1, replica_groups=mesh['batch'=4,'tm'=2,'space'=4] {'tm'}, dimensions={1} | all-to-all | bytes 2097152 | tf_op jit(solution)/shard_map/all_to_all | solution.py:68
  28.0 6.9 %fusion.30 = bf16[1,2,8,32,3072]{4,3,2,1,0:T(8,128)(2,1)S(1)} fusion(bf16[1024,3072]{1,0:T(8,128)(2,1)} %param.16, f32[2,8,32,1024]{3,2,1,0:T(8,128)} %bitcast.122, f32[1024]{0:T(1024)S(1)} %copy-done.8, f32[2,8,32]{2,1,0:T(8,128)S(1)} %rsqrt.20), kind=kOutput, calls=%fused_computation.36 | convolution fusion | flops 3224371200 | bytes 11540480 | tf_op jit(solution)/shard_map/dot_general | solution.py:72
  36.8 4.7 %collective-permute-start = (bf16[1,2,4,32,2048]{4,3,2,1,0:T(8,128)(2,1)}, bf16[1,2,4,32,2048]{4,3,2,1,0:T(8,128)(2,1)}, u32[]{:S(2)}, u32[]{:S(2)}) collective-permute-start(bf16[1,2,4,32,2048]{4,3,2,1,0:T(8,128)(2,1)} %get-tuple-element.133), channel_id=1, source_target_pairs={{0,1},{1,2},{2,3},{4,5},{5,6},{6,7},{8,9},{9,10},{10,11},{12,13},{... | collective-permute-start | bytes 3145736 | tf_op jit(solution)/shard_map/ppermute | solution.py:20
  46.0 16.4 %collective-permute-done = bf16[1,2,4,32,2048]{4,3,2,1,0:T(8,128)(2,1)} collective-permute-done((bf16[1,2,4,32,2048]{4,3,2,1,0:T(8,128)(2,1)}, bf16[1,2,4,32,2048]{4,3,2,1,0:T(8,128)(2,1)}, u32[]{:S(2)}, u32[]{:S(2)}) %collective-permute-start) | collective-permute-done | bytes 1048608 | tf_op jit(solution)/shard_map/ppermute | solution.py:20
  62.4 4.9 %collective-permute-done.1 = bf16[1,2,4,32,2048]{4,3,2,1,0:T(8,128)(2,1)} collective-permute-done((bf16[1,2,4,32,2048]{4,3,2,1,0:T(8,128)(2,1)S(1)}, bf16[1,2,4,32,2048]{4,3,2,1,0:T(8,128)(2,1)}, u32[]{:S(2)}, u32[]{:S(2)}) %collective-permute-start.1) | collective-permute-done | bytes 1048608 | tf_op jit(solution)/shard_map/ppermute | solution.py:21
  70.7 52.0 %while.11 = (s32[]{:T(128)}, bf16[2,256,1024]{1,2,0:T(8,128)(2,1)}, bf16[2,512,2048]{2,1,0:T(8,128)(2,1)}, s32[2]{0:T(128)S(1)}, bf16[2,256,1024]{2,1,0:T(8,128)...) while((s32[]{:T(128)}, bf16[2,256,1024]{1,2,0:T(8,128)(2,1)}, ...), condition=%wide.region_4.5_spmd.clone, body=%wide.region_1.4_spmd.clone.sunk | while | flops 550246912 | bytes 44339888 | solution.py:100
  75.3 3.9 %copy.117 = bf16[1,512,2048]{1,2,0:T(8,128)(2,1)} copy(bf16[1,512,2048]{2,1,0:T(8,128)(2,1)} %constant_dynamic-slice_fusion.4) | data formatting | bytes 4194304 | tf_op jit(solution)/shard_map/while/body/jit(dynamic_index_in_dim)/dynamic_slice | solution.py:100
  83.3 7.7 %fusion.90 = (f32[16,256]{1,0:T(8,128)S(1)}, f32[16,256,512]{2,1,0:T(8,128)}) fusion(pred[256,512]{1,0:T(8,128)(4,1)S(1)} %fusion.89, bf16[256,16,64]{0,2,1:T(8,128)(2,1)} %bitcast.111, bf16[512,16,64]{0,2,1:T(8,128)(2,1)} %bitcast.110), kind=kOutput, calls=%fused_computation.80.clone.1 | convolution fusion | flops 276824576 | bytes 10108928 | tf_op jit(solution)/shard_map/while/body/eval_jaxpr/sub | solution.py:35
  91.0 4.9 %fusion.91 = bf16[16,64,256]{2,1,0:T(8,128)(2,1)S(1)} fusion(bf16[512,16,64]{0,2,1:T(8,128)(2,1)S(1)} %bitcast.109, f32[16,256,512]{2,1,0:T(8,128)} %get-tuple-element.192, f32[16,256]{1,0:T(8,128)S(1)} %get-tuple-element.193), kind=kOutput, calls=%fused_computation.11.clone.1 | convolution fusion | flops 272891904 | bytes 9977856 | tf_op jit(solution)/shard_map/while/body/eval_jaxpr/hqk,khd->qhd/dot_general | solution.py:94
  101.3 3.9 %copy.117 = bf16[1,512,2048]{1,2,0:T(8,128)(2,1)} copy(bf16[1,512,2048]{2,1,0:T(8,128)(2,1)} %constant_dynamic-slice_fusion.4) | data formatting | bytes 4194304 | tf_op jit(solution)/shard_map/while/body/jit(dynamic_index_in_dim)/dynamic_slice | solution.py:100
  109.3 7.6 %fusion.90 = (f32[16,256]{1,0:T(8,128)S(1)}, f32[16,256,512]{2,1,0:T(8,128)}) fusion(pred[256,512]{1,0:T(8,128)(4,1)S(1)} %fusion.89, bf16[256,16,64]{0,2,1:T(8,128)(2,1)} %bitcast.111, bf16[512,16,64]{0,2,1:T(8,128)(2,1)} %bitcast.110), kind=kOutput, calls=%fused_computation.80.clone.1 | convolution fusion | flops 276824576 | bytes 10108928 | tf_op jit(solution)/shard_map/while/body/eval_jaxpr/sub | solution.py:35
  116.9 4.9 %fusion.91 = bf16[16,64,256]{2,1,0:T(8,128)(2,1)S(1)} fusion(bf16[512,16,64]{0,2,1:T(8,128)(2,1)S(1)} %bitcast.109, f32[16,256,512]{2,1,0:T(8,128)} %get-tuple-element.192, f32[16,256]{1,0:T(8,128)S(1)} %get-tuple-element.193), kind=kOutput, calls=%fused_computation.11.clone.1 | convolution fusion | flops 272891904 | bytes 9977856 | tf_op jit(solution)/shard_map/while/body/eval_jaxpr/hqk,khd->qhd/dot_general | solution.py:94
  126.9 6.6 %fusion.33 = bf16[1,2,256,3072]{3,2,1,0:T(8,128)(2,1)S(1)} fusion(bf16[1024,3072]{1,0:T(8,128)(2,1)} %param.19, bf16[2,256,1024]{2,1,0:T(8,128)(2,1)S(1)} %get-tuple-element.136, f32[1024]{0:T(1024)S(1)} %copy-done.9, f32[2,256]{1,0:T(2,128)S(1)} %add_rsqrt_fusion.1), kind=kOutput, calls=%fused_computation.37 | convolution fusion | flops 3224895488 | bytes 10491904 | tf_op jit(solution)/shard_map/dot_general | solution.py:115
  133.5 4.9 %copy.95 = bf16[1,2,256,3072]{3,1,0,2:T(2,128)(2,1)} copy(bf16[1,2,256,3072]{3,2,1,0:T(8,128)(2,1)S(1)} %fusion.33) | data formatting | bytes 6291456 | tf_op jit(solution)/shard_map/convert_element_type | solution.py:115
  138.4 5.3 %all-to-all-start.1 = ((bf16[1,2,256,3072]{3,1,0,2:T(2,128)(2,1)}), bf16[1,2,256,3072]{3,1,0,2:T(2,128)(2,1)}, u32[]{:S(2)}, u32[]{:S(2)}) async-start(bf16[1,2,256,3072]{3,1,0,2:T(2,128)(2,1)} %copy.95), calls=%async_computation.1 | async-start | bytes 6291456 | tf_op jit(solution)/shard_map/all_to_all | solution.py:118
  144.1 34.1 %all-to-all-done.1 = bf16[1,2,256,3072]{3,1,0,2:T(2,128)(2,1)} async-done(((bf16[1,2,256,3072]{3,1,0,2:T(2,128)(2,1)}), bf16[1,2,256,3072]{3,1,0,2:T(2,128)(2,1)}, u32[]{:S(2)}, u32[]{:S(2)}) %all-to-all-start.1) | async-done | bytes 3145760 | tf_op jit(solution)/shard_map/all_to_all | solution.py:118
  192.0 6.5 %fusion.64 = f32[128,16,4,4]{2,3,1,0:T(4,128)} fusion(bf16[4,128,16,64]{3,0,2,1:T(4,128)(2,1)} %copy.101, bf16[4,128,16,64]{3,0,2,1:T(4,128)(2,1)} %copy.102), kind=kOutput, calls=%fused_computation.83 | convolution fusion | flops 4194304 | bytes 2228224 | tf_op jit(solution)/shard_map/cfthd,cgthd->cthfg/dot_general | solution.py:45
  198.5 3.8 %copy.103 = f32[128,16,4,4]{0,1,3,2:T(8,128)S(1)} copy(f32[128,16,4,4]{2,3,1,0:T(4,128)} %fusion.64) | data formatting | bytes 262144 | tf_op jit(solution)/shard_map/cfthd,cgthd->cthfg/dot_general | solution.py:45
  202.5 4.3 %copy.105 = bf16[128,16,4,4]{3,2,1,0:T(4,128)(2,1)} copy(bf16[128,16,4,4]{0,1,3,2:T(8,128)(2,1)S(1)} %divide_convert_fusion.4) | data formatting | bytes 131072 | tf_op jit(solution)/shard_map/convert_element_type | solution.py:36
  211.4 5.9 %convert_bitcast_fusion = bf16[1,4,128,16,64]{4,1,3,2,0:T(4,128)(2,1)} fusion(bf16[4,128,16,64]{3,0,2,1:T(4,128)(2,1)} %copy.104, bf16[128,16,4,4]{3,2,1,0:T(4,128)(2,1)} %copy.105), kind=kOutput, calls=%fused_computation.49 | convolution fusion | flops 4718592 | bytes 2162688 | tf_op jit(solution)/shard_map/cthfg,cgthd->cfthd/dot_general | solution.py:50
  220.8 14.2 %all_to_all.43 = bf16[1,4,128,1024]{2,3,0,1:T(8,128)(2,1)} all-to-all(bf16[1,4,128,1024]{2,3,0,1:T(8,128)(2,1)S(1)} %bitcast.120), channel_id=1, replica_groups=mesh['batch'=4,'tm'=2,'space'=4] {'tm'}, dimensions={1} | all-to-all | bytes 2097152 | tf_op jit(solution)/shard_map/all_to_all | solution.py:126
  240.8 66.8 %reduce-scatter.2.cloned.1.call-done = bf16[128,1024]{1,0:T(8,128)(2,1)} async-done(((bf16[1024,1024]{1,0:T(8,128)(2,1)}), bf16[128,1024]{1,0:T(8,128)(2,1)}) %reduce-scatter.2.cloned.1.call-update) | async-done | bytes 262160 | tf_op jit(solution)/shard_map/reduce_scatter | solution.py:133
  307.7 4.1 %fusion.39 = bf16[2,256,1024]{2,1,0:T(8,128)(2,1)} fusion(bf16[2,256,1024]{2,1,0:T(8,128)(2,1)} %copy-done.12, bf16[2,256,1024]{2,1,0:T(8,128)(2,1)S(1)} %bitcast.126, bf16[1024,1024]{1,0:T(8,128)(2,1)} %param.20), kind=kOutput, calls=%fused_computation.44 | convolution fusion | flops 1075314688 | bytes 5242880 | tf_op jit(solution)/shard_map/dot_general | solution.py:129
  311.7 29.6 %all-reduce.2.cloned.1.call-done = bf16[128,1024]{1,0:T(8,128)(2,1)} async-done(((bf16[128,1024]{1,0:T(8,128)(2,1)}), bf16[128,1024]{1,0:T(8,128)(2,1)}) %all-reduce.2.cloned.1.call-update) | async-done | bytes 262160 | tf_op jit(solution)/shard_map/psum | solution.py:144
  (84 shorter events, 65.1 us)
Async XLA Ops:
  7.2 115.5 %copy-start = (bf16[1024,1024]{1,0:T(8,128)(2,1)S(1)}, bf16[1024,1024]{1,0:T(8,128)(2,1)}, u32[]{:S(2)}) copy-start(bf16[1024,1024]{1,0:T(8,128)(2,1)} %param.17) | copy-start | bytes 6291460
  26.0 2.0 copy-start.8
  34.9 1.9 copy-start.3
  36.8 25.6 %collective-permute-start = (bf16[1,2,4,32,2048]{4,3,2,1,0:T(8,128)(2,1)}, bf16[1,2,4,32,2048]{4,3,2,1,0:T(8,128)(2,1)}, u32[]{:S(2)}, u32[]{:S(2)}) collective-permute-start(bf16[1,2,4,32,2048]{4,3,2,1,0:T(8,128)(2,1)} %get-tuple-element.133), channel_id=1, source_target_pairs={{0,1},{1,2},{2,3},{4,5},{5,6},{6,7},{8,9},{9,10},{10,11},{12,13},{... | collective-permute-start | bytes 3145736 | tf_op jit(solution)/shard_map/ppermute | solution.py:20
  41.5 25.8 %collective-permute-start.1 = (bf16[1,2,4,32,2048]{4,3,2,1,0:T(8,128)(2,1)S(1)}, bf16[1,2,4,32,2048]{4,3,2,1,0:T(8,128)(2,1)}, u32[]{:S(2)}, u32[]{:S(2)}) collective-permute-start(bf16[1,2,4,32,2048]{4,3,2,1,0:T(8,128)(2,1)S(1)} %get-tuple-element.134), channel_id=1, source_target_pairs={{1,0},{2,1},{3,2},{5,4},{6,5},{7,6},{9,8},{10,9},{11,10},{13,12},{... | collective-permute-start | bytes 3145736 | tf_op jit(solution)/shard_map/ppermute | solution.py:21
  43.0 1.9 copy-start.4
  44.9 22.3 %slice-start = ((bf16[1,2,8,32,3072]{4,3,2,1,0:T(8,128)(2,1)}), bf16[1,2,8,32,2048]{4,3,2,1,0:T(8,128)(2,1)S(1)}, s32[]{:S(2)}) async-start(bf16[1,2,8,32,3072]{4,3,2,1,0:T(8,128)(2,1)} %copy-done.3), calls=%async_computation.6 | async-start | bytes 4194304 | tf_op jit(solution)/shard_map/slice | solution.py:75
  46.0 24.7 %copy-start.10 = (s32[1,2]{1,0:T(1,128)S(1)}, s32[1,2]{1,0:T(1,128)}, u32[]{:S(2)}) copy-start(s32[1,2]{1,0:T(1,128)} %param.14) | copy-start | bytes 28
  79.2 3.1 copy-start.2
  83.3 7.7 %copy-start.1 = (bf16[512,1024]{0,1:T(8,128)(2,1)S(1)}, bf16[512,1024]{0,1:T(8,128)(2,1)}, u32[]{:S(2)}) copy-start(bf16[512,1024]{0,1:T(8,128)(2,1)} %get-tuple-element.190) | copy-start | bytes 3145732 | tf_op jit(solution)/shard_map/while
  105.2 3.1 copy-start.2
  109.3 7.6 %copy-start.1 = (bf16[512,1024]{0,1:T(8,128)(2,1)S(1)}, bf16[512,1024]{0,1:T(8,128)(2,1)}, u32[]{:S(2)}) copy-start(bf16[512,1024]{0,1:T(8,128)(2,1)} %get-tuple-element.190) | copy-start | bytes 3145732 | tf_op jit(solution)/shard_map/while
  122.6 4.3 %copy-start.9 = (f32[1024]{0:T(1024)S(1)}, f32[1024]{0:T(1024)}, u32[]{:S(2)}) copy-start(f32[1024]{0:T(1024)} %param.18) | copy-start | bytes 12292
  125.9 1.0 copy-start.12
  138.4 5.6 %copy-start.11 = (s32[1,4]{1,0:T(1,128)S(1)}, s32[1,4]{1,0:T(1,128)}, u32[]{:S(2)}) copy-start(s32[1,4]{1,0:T(1,128)} %param.13) | copy-start | bytes 52
  138.4 39.8 %all-to-all-start.1 = ((bf16[1,2,256,3072]{3,1,0,2:T(2,128)(2,1)}), bf16[1,2,256,3072]{3,1,0,2:T(2,128)(2,1)}, u32[]{:S(2)}, u32[]{:S(2)}) async-start(bf16[1,2,256,3072]{3,1,0,2:T(2,128)(2,1)} %copy.95), calls=%async_computation.1 | async-start | bytes 6291456 | tf_op jit(solution)/shard_map/all_to_all | solution.py:118
  143.7 163.9 %reduce-scatter.2.cloned.1.call-start = ((), (), s32[]{:S(2)}) async-start(), calls=%async_computation.4 | async-start | bytes 2359296 | tf_op jit(solution)/shard_map/reduce_scatter | solution.py:133
  236.5 1.6 copy-start.7
  236.6 1.0 copy-start.5
  240.7 66.9 %copy-start.6 = (bf16[1,2,2,128,1024]{4,3,2,1,0:T(8,128)(2,1)S(1)}, bf16[1,2,2,128,1024]{4,3,2,1,0:T(8,128)(2,1)}, u32[]{:S(2)}) copy-start(bf16[1,2,2,128,1024]{4,3,2,1,0:T(8,128)(2,1)} %copy-done.5) | copy-start | bytes 3145732
  240.8 100.6 %all-reduce.2.cloned.1.call-start = ((), (), s32[]{:S(2)}) async-start(), calls=%async_computation.5 | async-start | bytes 524288 | tf_op jit(solution)/shard_map/psum | solution.py:144
Sparse Core Ops, SparseCore 0:
  240.9 66.6 reduce-scatter.1
  309.9 31.3 all-reduce.1
where the time goes:
time: 351 us; the launch traced here: 350 us
  waiting for transfers between devices  152 us (43%)
  local copies, waits for them, and re-layouts  70.6 us (20%)
  matrix products  60.8 us (17%)
  blocking collectives  33 us (9%)
  between operations  14.3 us (4%)
  starting transfers between devices  11.8 us (3%)
  other arithmetic  7.61 us (2%)
    reduce_scatter x1, waiting for transfers between devices, per_device(): lax.psum_scatter(lax.dot_general(flat_context, flat_cotangent, (((0,), (0...  66.8 us
    all_to_all x1, waiting for transfers between devices, per_device(): lax.all_to_all(projected_two, 'tm', split_axis=2, concat_axis=1, tiled=True)  34.1 us
    psum x1, waiting for transfers between devices, per_device(): weight_grad = lax.psum(own_rows, 'batch').astype(jnp.float32)  29.6 us
    all_to_all x1, blocking collectives, per_device(): lax.all_to_all(clip_tokens, 'tm', split_axis=1, concat_axis=3, tiled=True)  18.8 us
    dynamic_slice x10, local copies, waits for them, and re-layouts, per_device(): lax.map(spatial_item, (projected[..., :D].reshape(item_count, tokens, D),...  17.4 us
    ppermute x1, waiting for transfers between devices, extended(): before = lax.ppermute(last, axis, up)  16.4 us
    sub x2, matrix products, softmax_rounded(): exponent = jnp.exp(masked - top_score)  15.3 us
    all_to_all x1, blocking collectives, per_device(): lax.all_to_all(context_all, 'tm', split_axis=1, concat_axis=2, tiled=True)  14.2 us
  transfers between devices with their start and end apart: 5, of which 5 were waited for; matrix products, arithmetic and copies ran while one was open for 2% of the time, Pallas kernels for 0%

commit v1 on v0

--- a/solution.py
+++ b/solution.py
@@ -8,6 +8,12 @@
 HEADS = 16
 HEAD_DIM = 64
 floor_term = 0.5
+
+
+def summed_here(x, mesh_axis):
+    parts = lax.all_gather(x, mesh_axis, axis=0, tiled=False)
+    total = parts.sum(axis=0)
+    return total
 
 
 def extended(value, sides, width):
@@ -141,7 +147,7 @@
         scatter_dimension=0,
         tiled=True,
     )
-    weight_grad = lax.psum(own_rows, "batch").astype(jnp.float32)
+    weight_grad = summed_here(own_rows, "batch").astype(jnp.float32)
     return (output.reshape(clip_count, frame_count, row_count, col_count, D), weight_grad)
 
 

time: 351 us -> 335 us (0.954)
  waiting for transfers between devices: 152 us -> 135 us
    psum x1 -> x0, waiting for transfers between devices: 29.6 us -> none  [per_device(): weight_grad = lax.psum(own_rows, 'batch').astype(jnp.float32)]
    all_gather x0 -> x1, waiting for transfers between devices: none -> 13.2 us  [summed_here(): parts = lax.all_gather(x, mesh_axis, axis=0, tiled=False)]
where the time goes in v1:
time: 335 us; the launch traced here: 334 us
  waiting for transfers between devices  135 us (40%)
  local copies, waits for them, and re-layouts  70.6 us (21%)
  matrix products  60.8 us (18%)
  blocking collectives  33 us (10%)
  between operations  14.3 us (4%)
  starting transfers between devices  11.8 us (4%)
  other arithmetic  8.09 us (2%)
    reduce_scatter x1, waiting for transfers between devices, per_device(): lax.psum_scatter(lax.dot_general(flat_context, flat_cotangent, (((0,), (0...  66.8 us
    all_to_all x1, waiting for transfers between devices, per_device(): lax.all_to_all(projected_two, 'tm', split_axis=2, concat_axis=1, tiled=True)  34.1 us
    all_to_all x1, blocking collectives, per_device(): lax.all_to_all(clip_tokens, 'tm', split_axis=1, concat_axis=3, tiled=True)  18.8 us
    dynamic_slice x10, local copies, waits for them, and re-layouts, per_device(): lax.map(spatial_item, (projected[..., :D].reshape(item_count, tokens, D),...  17.4 us
    ppermute x1, waiting for transfers between devices, extended(): before = lax.ppermute(last, axis, up)  16.4 us
    sub x2, matrix products, softmax_rounded(): exponent = jnp.exp(masked - top_score)  15.3 us
    all_to_all x1, blocking collectives, per_device(): lax.all_to_all(context_all, 'tm', split_axis=1, concat_axis=2, tiled=True)  14.2 us
    all_gather x1, waiting for transfers between devices, summed_here(): parts = lax.all_gather(x, mesh_axis, axis=0, tiled=False)  13.2 us
  transfers between devices with their start and end apart: 5, of which 5 were waited for; matrix products, arithmetic and copies ran while one was open for 2% of the time, Pallas kernels for 0%

profile of v1, /device:TPU:0, one launch (start us, length us, event | category | flops | bytes accessed | tf_op | source)
XLA Modules:
  0.0 334.1 jit_solution(11115330257437554762)
XLA Ops:
  7.2 18.8 %all_to_all.42 = bf16[1,4,8,16,1024]{4,3,2,0,1:T(8,128)(2,1)S(1)} all-to-all(bf16[1,4,8,16,1024]{4,3,2,0,1:T(8,128)(2,1)} %bitcast.126), channel_id=1, replica_groups=mesh['batch'=4,'tm'=2,'space'=4] {'tm'}, dimensions={1} | all-to-all | bytes 2097152 | tf_op jit(solution)/shard_map/all_to_all | solution.py:74
  28.0 6.9 %fusion.30 = bf16[1,2,8,32,3072]{4,3,2,1,0:T(8,128)(2,1)S(1)} fusion(bf16[1024,3072]{1,0:T(8,128)(2,1)} %param.16, f32[2,8,32,1024]{3,2,1,0:T(8,128)} %bitcast.123, f32[1024]{0:T(1024)S(1)} %copy-done.8, f32[2,8,32]{2,1,0:T(8,128)S(1)} %rsqrt.20), kind=kOutput, calls=%fused_computation.36 | convolution fusion | flops 3224371200 | bytes 11540480 | tf_op jit(solution)/shard_map/dot_general | solution.py:78
  36.8 4.7 %collective-permute-start = (bf16[1,2,4,32,2048]{4,3,2,1,0:T(8,128)(2,1)}, bf16[1,2,4,32,2048]{4,3,2,1,0:T(8,128)(2,1)}, u32[]{:S(2)}, u32[]{:S(2)}) collective-permute-start(bf16[1,2,4,32,2048]{4,3,2,1,0:T(8,128)(2,1)} %get-tuple-element.133), channel_id=1, source_target_pairs={{0,1},{1,2},{2,3},{4,5},{5,6},{6,7},{8,9},{9,10},{10,11},{12,13},{... | collective-permute-start | bytes 3145736 | tf_op jit(solution)/shard_map/ppermute | solution.py:26
  46.0 16.4 %collective-permute-done = bf16[1,2,4,32,2048]{4,3,2,1,0:T(8,128)(2,1)} collective-permute-done((bf16[1,2,4,32,2048]{4,3,2,1,0:T(8,128)(2,1)}, bf16[1,2,4,32,2048]{4,3,2,1,0:T(8,128)(2,1)}, u32[]{:S(2)}, u32[]{:S(2)}) %collective-permute-start) | collective-permute-done | bytes 1048608 | tf_op jit(solution)/shard_map/ppermute | solution.py:26
  62.4 4.9 %collective-permute-done.1 = bf16[1,2,4,32,2048]{4,3,2,1,0:T(8,128)(2,1)} collective-permute-done((bf16[1,2,4,32,2048]{4,3,2,1,0:T(8,128)(2,1)S(1)}, bf16[1,2,4,32,2048]{4,3,2,1,0:T(8,128)(2,1)}, u32[]{:S(2)}, u32[]{:S(2)}) %collective-permute-start.1) | collective-permute-done | bytes 1048608 | tf_op jit(solution)/shard_map/ppermute | solution.py:27
  70.7 52.0 %while.11 = (s32[]{:T(128)}, bf16[2,256,1024]{1,2,0:T(8,128)(2,1)}, bf16[2,512,2048]{2,1,0:T(8,128)(2,1)}, s32[2]{0:T(128)S(1)}, bf16[2,256,1024]{2,1,0:T(8,128)...) while((s32[]{:T(128)}, bf16[2,256,1024]{1,2,0:T(8,128)(2,1)}, ...), condition=%wide.region_4.5_spmd.clone, body=%wide.region_1.4_spmd.clone.sunk | while | flops 550246912 | bytes 44339888 | solution.py:106
  75.3 3.9 %copy.117 = bf16[1,512,2048]{1,2,0:T(8,128)(2,1)} copy(bf16[1,512,2048]{2,1,0:T(8,128)(2,1)} %constant_dynamic-slice_fusion.4) | data formatting | bytes 4194304 | tf_op jit(solution)/shard_map/while/body/jit(dynamic_index_in_dim)/dynamic_slice | solution.py:106
  83.3 7.7 %fusion.90 = (f32[16,256]{1,0:T(8,128)S(1)}, f32[16,256,512]{2,1,0:T(8,128)}) fusion(pred[256,512]{1,0:T(8,128)(4,1)S(1)} %fusion.89, bf16[256,16,64]{0,2,1:T(8,128)(2,1)} %bitcast.112, bf16[512,16,64]{0,2,1:T(8,128)(2,1)} %bitcast.111), kind=kOutput, calls=%fused_computation.80.clone.1 | convolution fusion | flops 276824576 | bytes 10108928 | tf_op jit(solution)/shard_map/while/body/eval_jaxpr/sub | solution.py:41
  91.0 4.9 %fusion.91 = bf16[16,64,256]{2,1,0:T(8,128)(2,1)S(1)} fusion(bf16[512,16,64]{0,2,1:T(8,128)(2,1)S(1)} %bitcast.110, f32[16,256,512]{2,1,0:T(8,128)} %get-tuple-element.192, f32[16,256]{1,0:T(8,128)S(1)} %get-tuple-element.193), kind=kOutput, calls=%fused_computation.11.clone.1 | convolution fusion | flops 272891904 | bytes 9977856 | tf_op jit(solution)/shard_map/while/body/eval_jaxpr/hqk,khd->qhd/dot_general | solution.py:100
  101.3 3.9 %copy.117 = bf16[1,512,2048]{1,2,0:T(8,128)(2,1)} copy(bf16[1,512,2048]{2,1,0:T(8,128)(2,1)} %constant_dynamic-slice_fusion.4) | data formatting | bytes 4194304 | tf_op jit(solution)/shard_map/while/body/jit(dynamic_index_in_dim)/dynamic_slice | solution.py:106
  109.3 7.6 %fusion.90 = (f32[16,256]{1,0:T(8,128)S(1)}, f32[16,256,512]{2,1,0:T(8,128)}) fusion(pred[256,512]{1,0:T(8,128)(4,1)S(1)} %fusion.89, bf16[256,16,64]{0,2,1:T(8,128)(2,1)} %bitcast.112, bf16[512,16,64]{0,2,1:T(8,128)(2,1)} %bitcast.111), kind=kOutput, calls=%fused_computation.80.clone.1 | convolution fusion | flops 276824576 | bytes 10108928 | tf_op jit(solution)/shard_map/while/body/eval_jaxpr/sub | solution.py:41
  116.9 4.9 %fusion.91 = bf16[16,64,256]{2,1,0:T(8,128)(2,1)S(1)} fusion(bf16[512,16,64]{0,2,1:T(8,128)(2,1)S(1)} %bitcast.110, f32[16,256,512]{2,1,0:T(8,128)} %get-tuple-element.192, f32[16,256]{1,0:T(8,128)S(1)} %get-tuple-element.193), kind=kOutput, calls=%fused_computation.11.clone.1 | convolution fusion | flops 272891904 | bytes 9977856 | tf_op jit(solution)/shard_map/while/body/eval_jaxpr/hqk,khd->qhd/dot_general | solution.py:100
  126.9 6.6 %fusion.33 = bf16[1,2,256,3072]{3,2,1,0:T(8,128)(2,1)S(1)} fusion(bf16[1024,3072]{1,0:T(8,128)(2,1)} %param.19, bf16[2,256,1024]{2,1,0:T(8,128)(2,1)S(1)} %get-tuple-element.136, f32[1024]{0:T(1024)S(1)} %copy-done.9, f32[2,256]{1,0:T(2,128)S(1)} %add_rsqrt_fusion.1), kind=kOutput, calls=%fused_computation.37 | convolution fusion | flops 3224895488 | bytes 10491904 | tf_op jit(solution)/shard_map/dot_general | solution.py:121
  133.5 4.9 %copy.95 = bf16[1,2,256,3072]{3,1,0,2:T(2,128)(2,1)} copy(bf16[1,2,256,3072]{3,2,1,0:T(8,128)(2,1)S(1)} %fusion.33) | data formatting | bytes 6291456 | tf_op jit(solution)/shard_map/convert_element_type | solution.py:121
  138.4 5.3 %all-to-all-start.1 = ((bf16[1,2,256,3072]{3,1,0,2:T(2,128)(2,1)}), bf16[1,2,256,3072]{3,1,0,2:T(2,128)(2,1)}, u32[]{:S(2)}, u32[]{:S(2)}) async-start(bf16[1,2,256,3072]{3,1,0,2:T(2,128)(2,1)} %copy.95), calls=%async_computation.1 | async-start | bytes 6291456 | tf_op jit(solution)/shard_map/all_to_all | solution.py:124
  144.1 34.1 %all-to-all-done.1 = bf16[1,2,256,3072]{3,1,0,2:T(2,128)(2,1)} async-done(((bf16[1,2,256,3072]{3,1,0,2:T(2,128)(2,1)}), bf16[1,2,256,3072]{3,1,0,2:T(2,128)(2,1)}, u32[]{:S(2)}, u32[]{:S(2)}) %all-to-all-start.1) | async-done | bytes 3145760 | tf_op jit(solution)/shard_map/all_to_all | solution.py:124
  192.0 6.5 %fusion.64 = f32[128,16,4,4]{2,3,1,0:T(4,128)} fusion(bf16[4,128,16,64]{3,0,2,1:T(4,128)(2,1)} %copy.101, bf16[4,128,16,64]{3,0,2,1:T(4,128)(2,1)} %copy.102), kind=kOutput, calls=%fused_computation.83 | convolution fusion | flops 4194304 | bytes 2228224 | tf_op jit(solution)/shard_map/cfthd,cgthd->cthfg/dot_general | solution.py:51
  198.5 3.8 %copy.103 = f32[128,16,4,4]{0,1,3,2:T(8,128)S(1)} copy(f32[128,16,4,4]{2,3,1,0:T(4,128)} %fusion.64) | data formatting | bytes 262144 | tf_op jit(solution)/shard_map/cfthd,cgthd->cthfg/dot_general | solution.py:51
  202.5 4.3 %copy.105 = bf16[128,16,4,4]{3,2,1,0:T(4,128)(2,1)} copy(bf16[128,16,4,4]{0,1,3,2:T(8,128)(2,1)S(1)} %divide_convert_fusion.4) | data formatting | bytes 131072 | tf_op jit(solution)/shard_map/convert_element_type | solution.py:42
  211.4 5.9 %convert_bitcast_fusion = bf16[1,4,128,16,64]{4,1,3,2,0:T(4,128)(2,1)} fusion(bf16[4,128,16,64]{3,0,2,1:T(4,128)(2,1)} %copy.104, bf16[128,16,4,4]{3,2,1,0:T(4,128)(2,1)} %copy.105), kind=kOutput, calls=%fused_computation.49 | convolution fusion | flops 4718592 | bytes 2162688 | tf_op jit(solution)/shard_map/cthfg,cgthd->cfthd/dot_general | solution.py:56
  220.8 14.2 %all_to_all.43 = bf16[1,4,128,1024]{2,3,0,1:T(8,128)(2,1)} all-to-all(bf16[1,4,128,1024]{2,3,0,1:T(8,128)(2,1)S(1)} %bitcast.121), channel_id=1, replica_groups=mesh['batch'=4,'tm'=2,'space'=4] {'tm'}, dimensions={1} | all-to-all | bytes 2097152 | tf_op jit(solution)/shard_map/all_to_all | solution.py:132
  240.8 66.8 %reduce-scatter.2.cloned.1.call-done = bf16[128,1024]{1,0:T(8,128)(2,1)} async-done(((bf16[1024,1024]{1,0:T(8,128)(2,1)}), bf16[128,1024]{1,0:T(8,128)(2,1)}) %reduce-scatter.2.cloned.1.call-update) | async-done | bytes 262160 | tf_op jit(solution)/shard_map/reduce_scatter | solution.py:139
  307.7 4.1 %fusion.39 = bf16[2,256,1024]{2,1,0:T(8,128)(2,1)} fusion(bf16[2,256,1024]{2,1,0:T(8,128)(2,1)} %copy-done.12, bf16[2,256,1024]{2,1,0:T(8,128)(2,1)S(1)} %bitcast.128, bf16[1024,1024]{1,0:T(8,128)(2,1)} %param.20), kind=kOutput, calls=%fused_computation.44 | convolution fusion | flops 1075314688 | bytes 5242880 | tf_op jit(solution)/shard_map/dot_general | solution.py:135
  311.7 13.2 %all-gather.3.cloned.1.call-done = bf16[512,1024]{1,0:T(8,128)(2,1)} async-done(((bf16[128,1024]{1,0:T(8,128)(2,1)}), bf16[512,1024]{1,0:T(8,128)(2,1)}) %all-gather.3.cloned.1.call-update) | async-done | bytes 1048592 | tf_op jit(solution)/shard_map/all_gather | solution.py:14
  (85 shorter events, 65.6 us)
Async XLA Ops:
  7.2 115.5 %copy-start = (bf16[1024,1024]{1,0:T(8,128)(2,1)S(1)}, bf16[1024,1024]{1,0:T(8,128)(2,1)}, u32[]{:S(2)}) copy-start(bf16[1024,1024]{1,0:T(8,128)(2,1)} %param.17) | copy-start | bytes 6291460
  26.0 2.0 copy-start.8
  34.9 1.9 copy-start.3
  36.8 25.6 %collective-permute-start = (bf16[1,2,4,32,2048]{4,3,2,1,0:T(8,128)(2,1)}, bf16[1,2,4,32,2048]{4,3,2,1,0:T(8,128)(2,1)}, u32[]{:S(2)}, u32[]{:S(2)}) collective-permute-start(bf16[1,2,4,32,2048]{4,3,2,1,0:T(8,128)(2,1)} %get-tuple-element.133), channel_id=1, source_target_pairs={{0,1},{1,2},{2,3},{4,5},{5,6},{6,7},{8,9},{9,10},{10,11},{12,13},{... | collective-permute-start | bytes 3145736 | tf_op jit(solution)/shard_map/ppermute | solution.py:26
  41.5 25.8 %collective-permute-start.1 = (bf16[1,2,4,32,2048]{4,3,2,1,0:T(8,128)(2,1)S(1)}, bf16[1,2,4,32,2048]{4,3,2,1,0:T(8,128)(2,1)}, u32[]{:S(2)}, u32[]{:S(2)}) collective-permute-start(bf16[1,2,4,32,2048]{4,3,2,1,0:T(8,128)(2,1)S(1)} %get-tuple-element.134), channel_id=1, source_target_pairs={{1,0},{2,1},{3,2},{5,4},{6,5},{7,6},{9,8},{10,9},{11,10},{13,12},{... | collective-permute-start | bytes 3145736 | tf_op jit(solution)/shard_map/ppermute | solution.py:27
  43.0 1.9 copy-start.4
  44.9 22.3 %slice-start = ((bf16[1,2,8,32,3072]{4,3,2,1,0:T(8,128)(2,1)}), bf16[1,2,8,32,2048]{4,3,2,1,0:T(8,128)(2,1)S(1)}, s32[]{:S(2)}) async-start(bf16[1,2,8,32,3072]{4,3,2,1,0:T(8,128)(2,1)} %copy-done.3), calls=%async_computation.6 | async-start | bytes 4194304 | tf_op jit(solution)/shard_map/slice | solution.py:81
  46.0 24.7 %copy-start.10 = (s32[1,2]{1,0:T(1,128)S(1)}, s32[1,2]{1,0:T(1,128)}, u32[]{:S(2)}) copy-start(s32[1,2]{1,0:T(1,128)} %param.14) | copy-start | bytes 28
  79.2 3.1 copy-start.2
  83.3 7.7 %copy-start.1 = (bf16[512,1024]{0,1:T(8,128)(2,1)S(1)}, bf16[512,1024]{0,1:T(8,128)(2,1)}, u32[]{:S(2)}) copy-start(bf16[512,1024]{0,1:T(8,128)(2,1)} %get-tuple-element.190) | copy-start | bytes 3145732 | tf_op jit(solution)/shard_map/while
  105.2 3.1 copy-start.2
  109.3 7.6 %copy-start.1 = (bf16[512,1024]{0,1:T(8,128)(2,1)S(1)}, bf16[512,1024]{0,1:T(8,128)(2,1)}, u32[]{:S(2)}) copy-start(bf16[512,1024]{0,1:T(8,128)(2,1)} %get-tuple-element.190) | copy-start | bytes 3145732 | tf_op jit(solution)/shard_map/while
  122.6 4.3 %copy-start.9 = (f32[1024]{0:T(1024)S(1)}, f32[1024]{0:T(1024)}, u32[]{:S(2)}) copy-start(f32[1024]{0:T(1024)} %param.18) | copy-start | bytes 12292
  125.9 1.0 copy-start.12
  138.4 5.6 %copy-start.11 = (s32[1,4]{1,0:T(1,128)S(1)}, s32[1,4]{1,0:T(1,128)}, u32[]{:S(2)}) copy-start(s32[1,4]{1,0:T(1,128)} %param.13) | copy-start | bytes 52
  138.4 39.8 %all-to-all-start.1 = ((bf16[1,2,256,3072]{3,1,0,2:T(2,128)(2,1)}), bf16[1,2,256,3072]{3,1,0,2:T(2,128)(2,1)}, u32[]{:S(2)}, u32[]{:S(2)}) async-start(bf16[1,2,256,3072]{3,1,0,2:T(2,128)(2,1)} %copy.95), calls=%async_computation.1 | async-start | bytes 6291456 | tf_op jit(solution)/shard_map/all_to_all | solution.py:124
  143.7 163.9 %reduce-scatter.2.cloned.1.call-start = ((), (), s32[]{:S(2)}) async-start(), calls=%async_computation.4 | async-start | bytes 2359296 | tf_op jit(solution)/shard_map/reduce_scatter | solution.py:139
  236.5 1.6 copy-start.7
  236.6 1.0 copy-start.5
  240.7 66.9 %copy-start.6 = (bf16[1,2,2,128,1024]{4,3,2,1,0:T(8,128)(2,1)S(1)}, bf16[1,2,2,128,1024]{4,3,2,1,0:T(8,128)(2,1)}, u32[]{:S(2)}) copy-start(bf16[1,2,2,128,1024]{4,3,2,1,0:T(8,128)(2,1)} %copy-done.5) | copy-start | bytes 3145732
  240.8 84.2 %all-gather.3.cloned.1.call-start = ((), (), s32[]{:S(2)}) async-start(), calls=%async_computation.5 | async-start | bytes 1310720 | tf_op jit(solution)/shard_map/all_gather | solution.py:14
Sparse Core Ops, SparseCore 0:
  240.9 66.6 reduce-scatter.1
  309.2 15.7 all-gather.2
